TPU v7x, 256 devices: a whole 4x4x8 slice. The times are simulated.
256 devices in a mesh: grp: 32 (over y, z_lo, core), dev: 8 (over x, z_hi).
Axes of the slice: x: 4, y: 4, z: 8 (z_hi: 2, z_lo: 4; z = z_hi * 4 + z_lo), core: 2. Of those that a mesh axis runs over, the one named last changes fastest.
Arguments:
- stack: bfloat16 [608, 256, 2048], P('grp', None, 'dev'), may hold values from -12 to 12
- network: int32 [608, 2], replicated, may hold values from 0 to 149, as said below
- bands: int32 [149], replicated, may hold values from 1 to 8
Outputs:
- deramped: bfloat16 [149, 256, 2048], P(None, 'grp', 'dev')
- misfit: float32 [256, 2048], P('grp', 'dev')
- spectrum: float32 [2, 149, 15, 15], replicated
Inputs may be any that keep to these rules, and one draw needn't show every extreme that they name: `network`: each row holds a reference date and a later secondary date, both below 150; every pair of consecutive dates is some row.
All inputs are finite; a program needn't handle non-finite values.
Results may differ from a plain program's by a relative error of at most 0.005.
Values may be sent and summed in bfloat16 or wider, within the bound.
No kernel may reach another device: no remote copies, remote signals or barrier semaphores. Data moves between devices by JAX's collectives and lax.ppermute only.
A program may use at most 128 MiB of HBM per device.

v0:
```python
import math
import jax
import jax.numpy as jnp
import numpy as np
from jax import lax
from jax.sharding import PartitionSpec as P

BAND = 8
FREQS = 2 * BAND - 1
HIGH = lax.Precision.HIGHEST


def design_of(network, solved):
    dates = jnp.arange(1, solved + 1, dtype=jnp.int32)
    return (network[:, 1:2] == dates[None, :]).astype(jnp.float32) - (
        network[:, 0:1] == dates[None, :]
    ).astype(jnp.float32)


def build_inverse(network, solved):
    design = design_of(network, solved)
    normal = jnp.dot(design.T, design, precision=HIGH)
    factor = jnp.linalg.cholesky(normal)
    pinv = jax.scipy.linalg.cho_solve((factor, True), design.T)
    return (pinv.astype(jnp.bfloat16), design.astype(jnp.bfloat16))


def basis(positions, length):
    index = jnp.arange(FREQS, dtype=jnp.int32)
    step = jnp.where(index < BAND, index, index - (BAND - 1))
    turns = positions[:, None] * step[None, :] % length
    angle = turns.astype(jnp.float32) * (2.0 * math.pi / length)
    return jnp.where(index[None, :] < BAND, jnp.cos(angle), jnp.sin(angle))


def mirror():
    out = np.zeros((FREQS, FREQS, 2, FREQS, FREQS), np.float32)
    for k in range(FREQS):
        for l in range(FREQS):
            fk, fl = (k - (BAND - 1), l - (BAND - 1))
            ck, cl = (abs(fk), abs(fl))
            sk, sl = (abs(fk) + BAND - 1, abs(fl) + BAND - 1)
            gk, gl = (np.sign(fk), np.sign(fl))
            out[k, l, 0, ck, cl] += 1
            if gk * gl:
                out[k, l, 0, sk, sl] -= gk * gl
            if gk:
                out[k, l, 1, sk, cl] -= gk
            if gl:
                out[k, l, 1, ck, sl] -= gl
    return out.reshape(FREQS * FREQS * 2, FREQS * FREQS)


def on_device(stack, network, bands):
    solved = bands.shape[0]
    groups = lax.axis_size("grp")
    held, rows_all, col_dev = stack.shape
    row_dev = rows_all // groups
    cols_all = col_dev * lax.axis_size("dev")
    pixels = row_dev * col_dev
    packed = stack.reshape(held, groups, row_dev, col_dev).transpose(1, 0, 2, 3)
    block = lax.all_to_all(packed, "grp", 0, 0, tiled=True)
    rows = basis(jnp.arange(rows_all, dtype=jnp.int32), rows_all)
    cols = basis(lax.axis_index("dev") * col_dev + jnp.arange(col_dev, dtype=jnp.int32), cols_all)
    wide = stack.astype(jnp.float32)
    half = jnp.einsum("ihw,ha->iaw", wide, rows, precision=HIGH)
    local = jnp.einsum("iaw,wb->iab", half, cols, precision=HIGH)
    local = local.reshape(held, FREQS * FREQS)
    summed = lax.psum(local, "dev")
    every = lax.all_gather(summed, "grp", axis=0, tiled=True)
    pinv, design = build_inverse(network, solved)
    scale = 1.0 / (rows_all * cols_all)
    coef = scale * lax.dot_general(
        every, pinv.astype(jnp.float32), (((0,), (1,)), ((), ())), precision=HIGH
    )
    index = np.arange(FREQS)
    step = np.where(index < BAND, index, index - (BAND - 1))
    weight = np.where(step == 0, 1.0, 2.0)
    kmax = np.maximum(step[:, None], step[None, :]).reshape(-1)
    both = (weight[:, None] * weight[None, :]).reshape(-1).astype(np.float32)
    masked = jnp.where(jnp.asarray(kmax)[:, None] < bands[None, :], coef, 0.0)
    signed = jnp.dot(jnp.asarray(mirror()), masked, precision=HIGH)
    spectrum = signed.reshape(FREQS, FREQS, 2, solved).transpose(2, 3, 0, 1)
    row_here = basis(
        lax.axis_index("grp") * row_dev + jnp.arange(row_dev, dtype=jnp.int32), rows_all
    )
    waves = (row_here.T[:, None, :, None] * cols.T[None, :, None, :]).reshape(FREQS * FREQS, pixels)
    ramp = lax.dot_general(
        masked * jnp.asarray(both)[:, None], waves, (((0,), (0,)), ((), ())), precision=HIGH
    )
    flat = block.reshape(held * groups, pixels)
    series = jnp.dot(pinv, flat, preferred_element_type=jnp.float32)
    deramped = (series - ramp).astype(jnp.bfloat16).reshape(solved, row_dev, col_dev)
    model = jnp.dot(design, series.astype(jnp.bfloat16), preferred_element_type=jnp.float32)
    resid = flat.astype(jnp.float32) - model
    misfit = jnp.sqrt(jnp.mean(resid * resid, axis=0) + 1e-06).reshape(row_dev, col_dev)
    return (deramped, misfit, spectrum)


def solution(mesh):
    return jax.shard_map(
        on_device,
        mesh=mesh,
        in_specs=(P("grp", None, "dev"), P(), P()),
        out_specs=(P(None, "grp", "dev"), P("grp", "dev"), P()),
        check_vma=False,
    )
```

profile of v0, /device:TPU:1, one launch (start us, length us, event | category | flops | bytes accessed | tf_op | source)
XLA Modules:
  0.0 182.2 jit_solution(6894326143020125078)
XLA Ops:
  0.6 0.0 copy-start
  0.6 1.7 copy-done
  2.3 1.6 copy_bitcast_fusion
  4.0 10.4 %all-to-all-start = ((bf16[32,19,8,256]{3,2,1,0:T(8,128)(2,1)}), bf16[32,19,8,256]{3,2,1,0:T(8,128)(2,1)}, u32[]{:S(2)}, u32[]{:S(2)}) async-start(bf16[32,19,8,256]{3,2,1,0:T(8,128)(2,1)} %copy_bitcast_fusion), calls=%async_computation | async-start | bytes 4980736 | tf_op jit(solution)/shard_map/all_to_all | solution.py:62
  14.4 1.5 fusion.4
  15.9 0.1 copy.17
  16.1 11.7 %cholesky.51 = f32[128,128]{1,0:T(8,128)S(1)} custom-call(f32[128,128]{1,0:T(8,128)S(1)} %cholesky.124), custom_call_target="Cholesky" | custom-call | tf_op jit(solution)/shard_map/jit(cholesky)/cholesky | solution.py:23
  27.8 9.8 %custom-call.18 = f32[1,128,128]{1,2,0:T(8,128)S(1)} custom-call(f32[1,128,128]{2,1,0:T(8,128)S(1)} %get-tuple-element.26), custom_call_target="InvertDiagBlocksLowerTriangular" | custom-call | tf_op jit(solution)/shard_map/jit(cholesky)/cholesky | solution.py:23
  37.7 0.2 constant_dynamic-update-slice_fusion.1
  37.8 0.2 convolution_subtract_fusion.3
  38.0 1.9 %cholesky.110 = f32[21,21]{1,0:T(8,128)S(1)} custom-call(f32[21,21]{1,0:T(8,128)S(1)} %convolution_subtract_fusion.3), custom_call_target="Cholesky" | custom-call | tf_op jit(solution)/shard_map/jit(cholesky)/cholesky | solution.py:23
  39.9 0.6 compare_reduce_fusion
  40.6 0.6 compare_reduce_fusion.1
  42.6 0.1 fusion.20
  42.7 19.9 %custom-call.19 = f32[2,128,128]{1,2,0:T(8,128)S(1)} custom-call(f32[2,128,128]{2,1,0:T(8,128)S(1)} %pad_maximum_fusion.3), custom_call_target="InvertDiagBlocksLowerTriangular" | custom-call | tf_op jit(solution)/shard_map/jit(_cho_solve)/triangular_solve | solution.py:24
  62.6 0.1 convert_subtract_fusion.2
  62.7 0.7 fusion.7
  63.4 0.7 copy-done.2
  64.2 0.4 convolution_subtract_fusion.2
  64.6 0.3 fusion.53
  64.8 0.2 fusion.82
  65.0 0.2 copy.18
  65.3 1.2 convolution_bitcast_fusion
  66.5 0.5 fusion.32
  67.0 0.1 reshape.205
  67.1 45.8 %psum.7 = f32[19,225]{1,0:T(8,128)S(1)} all-reduce(f32[19,225]{1,0:T(8,128)S(1)} %reshape.205), channel_id=1, replica_groups=mesh['grp'=32,'dev'=8] {'dev'}, use_global_device_ids=true, to_apply=%region_4.5 | all-reduce | flops 4275 | bytes 34200 | tf_op jit(solution)/shard_map/psum | solution.py:69
  112.9 53.9 %all-gather = f32[32,19,225]{2,1,0:T(8,128)S(1)} all-gather(f32[1,19,225]{2,1,0:T(8,128)S(1)} %bitcast.72), channel_id=1, replica_groups=mesh['grp'=32,'dev'=8] {'grp'}, dimensions={0}, use_global_device_ids=true | all-gather | bytes 564300 | tf_op jit(solution)/shard_map/all_gather | solution.py:70
  166.8 0.9 reshape.238
  167.7 0.1 sine_select_fusion.1
  167.8 0.2 sine_select_fusion
  168.0 0.2 broadcast_multiply_fusion
  168.2 0.1 pad.23
  168.4 0.0 copy-start.12
  168.4 0.0 copy-start.5
  168.4 2.1 %copy.23 = f32[29,8,8,256]{3,1,2,0:T(8,128)} copy(f32[29,8,8,256]{3,2,1,0:T(8,128)S(1)} %bitcast.67) | data formatting | bytes 3801088
  170.5 1.4 convolution_subtract_fusion.1
  171.9 0.4 convolution_convert_fusion
  172.3 0.5 fusion.1
  172.9 0.5 fusion.83
  173.4 1.0 reshape.207
  174.5 2.5 %copy.22 = bf16[76,8,8,256]{3,1,2,0:T(8,128)(2,1)S(1)} copy(bf16[76,8,8,256]{3,2,1,0:T(8,128)(2,1)} %bitcast.15) | data formatting | bytes 4980736
  177.0 0.7 fusion.16
  177.7 1.0 multiply_reduce_fusion
  178.7 0.5 copy-done.1
  179.2 1.3 fusion
  180.5 0.1 copy.24
  180.7 0.9 slice.94
  181.6 0.6 sqrt.8
  (38 shorter events, 0.3 us)
Async XLA Ops:
  0.6 1.7 copy-start
  4.0 10.4 %copy-start.9 = (s32[608,2]{0,1:T(2,128)S(1)}, s32[608,2]{0,1:T(2,128)}, u32[]{:S(2)}) copy-start(s32[608,2]{0,1:T(2,128)} %param.7) | copy-start | bytes 14596
  4.0 170.5 %all-to-all-start = ((bf16[32,19,8,256]{3,2,1,0:T(8,128)(2,1)}), bf16[32,19,8,256]{3,2,1,0:T(8,128)(2,1)}, u32[]{:S(2)}, u32[]{:S(2)}) async-start(bf16[32,19,8,256]{3,2,1,0:T(8,128)(2,1)} %copy_bitcast_fusion), calls=%async_computation | async-start | bytes 4980736 | tf_op jit(solution)/shard_map/all_to_all | solution.py:62
  42.5 23.9 %copy-start.6 = (f32[149,149]{1,0:T(8,128)}, f32[149,149]{1,0:T(8,128)S(1)}, u32[]{:S(2)}) copy-start(f32[149,149]{1,0:T(8,128)S(1)} %select_select_fusion) | copy-start | bytes 266416
  62.6 2.7 %copy-start.7 = (f32[2,128,128]{1,2,0:T(8,128)}, f32[2,128,128]{1,2,0:T(8,128)S(1)}, u32[]{:S(2)}) copy-start(f32[2,128,128]{1,2,0:T(8,128)S(1)} %custom-call.19) | copy-start | bytes 393220
  63.4 0.7 copy-start.2
  168.3 2.2 %copy-start.3 = (f32[128,608]{0,1:T(8,128)S(1)}, f32[128,608]{0,1:T(8,128)}, u32[]{:S(2)}) copy-start(f32[128,608]{0,1:T(8,128)} %copy-done.2) | copy-start | bytes 933892
  168.3 3.5 %copy-start.8 = (f32[2,128,128]{1,2,0:T(8,128)S(1)}, f32[2,128,128]{1,2,0:T(8,128)}, u32[]{:S(2)}) copy-start(f32[2,128,128]{1,2,0:T(8,128)} %copy-done.7) | copy-start | bytes 393220
  168.4 4.0 %copy-start.4 = (f32[608,225]{1,0:T(8,128)S(1)}, f32[608,225]{1,0:T(8,128)}, u32[]{:S(2)}) copy-start(f32[608,225]{1,0:T(8,128)} %reshape.238) | copy-start | bytes 1641604
  168.4 4.0 %copy-start.11 = (s32[149]{0:T(256)S(1)}, s32[149]{0:T(256)}, u32[]{:S(2)}) copy-start(s32[149]{0:T(256)} %param.8) | copy-start | bytes 1792
  168.4 4.0 %copy-start.12 = (s32[225]{0:T(256)S(1)}, s32[225]{0:T(256)}, u32[]{:S(2)}) copy-start(s32[225]{0:T(256)} %constant.175.clone) | copy-start | bytes 2704
  168.4 4.5 %copy-start.5 = (f32[450,225]{1,0:T(8,128)S(1)}, f32[450,225]{1,0:T(8,128)}, u32[]{:S(2)}) copy-start(f32[450,225]{1,0:T(8,128)} %constant.176.clone) | copy-start | bytes 1215004
  177.7 1.5 copy-start.1
  177.7 1.5 copy-start.10
where the time goes:
time: 183 us; the launch traced here: 182 us
  blocking collectives  99.7 us (54%)
  other arithmetic  45.4 us (25%)
  local copies, waits for them, and re-layouts  13.4 us (7%)
  matrix products  11 us (6%)
  starting transfers between devices  10.4 us (6%)
  between operations  2.38 us (1%)
    all_gather x1, blocking collectives, on_device(): every = lax.all_gather(summed, 'grp', axis=0, tiled=True)  53.9 us
    psum x1, blocking collectives, on_device(): summed = lax.psum(local, 'dev')  45.8 us
    another operation x7, other arithmetic, build_inverse(): factor = jnp.linalg.cholesky(normal)  24.8 us
    another operation x6, other arithmetic, build_inverse(): pinv = jax.scipy.linalg.cho_solve((factor, True), design.T)  20 us
    all_to_all x1, starting transfers between devices, on_device(): block = lax.all_to_all(packed, 'grp', 0, 0, tiled=True)  10.4 us
    unnamed x31, local copies, waits for them, and re-layouts  8.8 us
  transfers between devices with their start and end apart: 1, of which 0 were waited for; matrix products, arithmetic and copies ran while one was open for 32% of the time, Pallas kernels for 0%

commit v1 on v0

--- a/solution.py
+++ b/solution.py
@@ -1,13 +1,24 @@
+import functools
 import math
 import jax
 import jax.numpy as jnp
 import numpy as np
 from jax import lax
 from jax.sharding import PartitionSpec as P
+from jax.lax import all_to_all, axis_size
 
 BAND = 8
 FREQS = 2 * BAND - 1
 HIGH = lax.Precision.HIGHEST
+
+
+def object_return_all(raw, lane_axis):
+    part_now = jnp.stack([raw for _ in range(axis_size(lane_axis))], axis=0)
+    carry_out = all_to_all(part_now, lane_axis, 0, 0)
+    return jnp.concatenate(carry_out, 0)
+
+
+sample_carry = functools.partial(object_return_all, lane_axis="grp")
 
 
 def design_of(network, solved):
@@ -67,7 +78,7 @@
     local = jnp.einsum("iaw,wb->iab", half, cols, precision=HIGH)
     local = local.reshape(held, FREQS * FREQS)
     summed = lax.psum(local, "dev")
-    every = lax.all_gather(summed, "grp", axis=0, tiled=True)
+    every = sample_carry(summed)
     pinv, design = build_inverse(network, solved)
     scale = 1.0 / (rows_all * cols_all)
     coef = scale * lax.dot_general(

time: 183 us -> 170 us (0.929)
  blocking collectives: 99.7 us -> 49.3 us
  waiting for transfers between devices: 0.01 us -> 18.3 us
  starting transfers between devices: 10.4 us -> 18.7 us
  matrix products: 11 us -> 16 us
  other arithmetic: 45.4 us -> 48.4 us
  local copies, waits for them, and re-layouts: 13.4 us -> 16.2 us
    all_gather x1 -> x0, blocking collectives: 53.9 us -> none  [on_device(): every = lax.all_gather(summed, 'grp', axis=0, tiled=True)]
    all_to_all x0 -> x1, waiting for transfers between devices: none -> 18.3 us  [object_return_all(): carry_out = all_to_all(part_now, lane_axis, 0, 0)]
    all_to_all x0 -> x1, starting transfers between devices: none -> 13.9 us  [object_return_all(): carry_out = all_to_all(part_now, lane_axis, 0, 0)]
    all_to_all x1, starting transfers between devices: 10.4 us -> 4.76 us  [on_device(): block = lax.all_to_all(packed, 'grp', 0, 0, tiled=True)]
    psum x1, blocking collectives: 45.8 us -> 49.3 us  [on_device(): summed = lax.psum(local, 'dev')]
    unnamed x31 -> x36, local copies, waits for them, and re-layouts: 8.8 us -> 9.15 us
  transfers between devices with their start and end apart: 1 -> 2, of which waited for: 0 -> 1; matrix products, arithmetic and copies ran while one was open for 32% -> 39% of each run, Pallas kernels for 0% -> 0%
where the time goes in v1:
time: 170 us; the launch traced here: 169 us
  blocking collectives  49.3 us (29%)
  other arithmetic  48.4 us (28%)
  starting transfers between devices  18.7 us (11%)
  waiting for transfers between devices  18.3 us (11%)
  local copies, waits for them, and re-layouts  16.2 us (10%)
  matrix products  16 us (9%)
  between operations  2.36 us (1%)
    psum x1, blocking collectives, on_device(): summed = lax.psum(local, 'dev')  49.3 us
    another operation x7, other arithmetic, build_inverse(): factor = jnp.linalg.cholesky(normal)  25.4 us
    another operation x6, other arithmetic, build_inverse(): pinv = jax.scipy.linalg.cho_solve((factor, True), design.T)  20 us
    all_to_all x1, waiting for transfers between devices, object_return_all(): carry_out = all_to_all(part_now, lane_axis, 0, 0)  18.3 us
    all_to_all x1, starting transfers between devices, object_return_all(): carry_out = all_to_all(part_now, lane_axis, 0, 0)  13.9 us
    unnamed x36, local copies, waits for them, and re-layouts  9.15 us
    all_to_all x1, starting transfers between devices, on_device(): block = lax.all_to_all(packed, 'grp', 0, 0, tiled=True)  4.76 us
    another operation x6, matrix products, build_inverse(): pinv = jax.scipy.linalg.cho_solve((factor, True), design.T)  4.73 us
  transfers between devices with their start and end apart: 2, of which 1 were waited for; matrix products, arithmetic and copies ran while one was open for 39% of the time, Pallas kernels for 0%

profile of v1, /device:TPU:1, one launch (start us, length us, event | category | flops | bytes accessed | tf_op | source)
XLA Modules:
  0.0 169.3 jit_solution(4474578592433351477)
XLA Ops:
  0.7 1.7 copy-done
  2.3 1.2 convolution_bitcast_fusion
  3.5 0.5 fusion.32
  4.2 49.3 %psum.7 = f32[19,225]{1,0:T(8,128)S(1)} all-reduce(f32[19,225]{1,0:T(8,128)S(1)} %reshape.210), channel_id=1, replica_groups=mesh['grp'=32,'dev'=8] {'dev'}, use_global_device_ids=true, to_apply=%region_4.5 | all-reduce | flops 4275 | bytes 34200 | tf_op jit(solution)/shard_map/psum | solution.py:80
  53.5 0.9 stack.2
  54.4 13.9 %all-to-all-start.1 = ((f32[32,19,225]{2,1,0:T(8,128)}), f32[32,19,225]{2,1,0:T(8,128)S(1)}, u32[]{:S(2)}, u32[]{:S(2)}) async-start(f32[32,19,225]{2,1,0:T(8,128)} %stack.2), calls=%async_computation.1 | async-start | bytes 1572864 | tf_op jit(solution)/shard_map/all_to_all | solution.py:17
  68.4 1.5 fusion.4
  69.9 0.8 copy.13
  70.7 1.6 copy_bitcast_fusion
  72.3 18.3 %all-to-all-done.1 = f32[32,19,225]{2,1,0:T(8,128)S(1)} async-done(((f32[32,19,225]{2,1,0:T(8,128)}), f32[32,19,225]{2,1,0:T(8,128)S(1)}, u32[]{:S(2)}, u32[]{:S(2)}) %all-to-all-start.1) | async-done | bytes 547232 | tf_op jit(solution)/shard_map/all_to_all | solution.py:17
  90.6 4.8 %all-to-all-start = ((bf16[32,19,8,256]{3,2,1,0:T(8,128)(2,1)}), bf16[32,19,8,256]{3,2,1,0:T(8,128)(2,1)}, u32[]{:S(2)}, u32[]{:S(2)}) async-start(bf16[32,19,8,256]{3,2,1,0:T(8,128)(2,1)} %copy_bitcast_fusion), calls=%async_computation | async-start | bytes 4980736 | tf_op jit(solution)/shard_map/all_to_all | solution.py:73
  95.4 0.9 fusion.17
  96.4 0.7 copy-done.6
  97.0 11.7 %cholesky.51 = f32[128,128]{1,0:T(8,128)S(1)} custom-call(f32[128,128]{1,0:T(8,128)S(1)} %cholesky.124), custom_call_target="Cholesky" | custom-call | tf_op jit(solution)/shard_map/jit(cholesky)/cholesky | solution.py:34
  108.8 10.4 %custom-call.18 = f32[1,128,128]{1,2,0:T(8,128)} custom-call(f32[1,128,128]{2,1,0:T(8,128)S(1)} %get-tuple-element.26), custom_call_target="InvertDiagBlocksLowerTriangular" | custom-call | tf_op jit(solution)/shard_map/jit(cholesky)/cholesky | solution.py:34
  119.2 1.0 constant_dynamic-update-slice_fusion.1
  120.3 0.9 convolution_subtract_fusion.3
  121.1 1.9 %cholesky.110 = f32[21,21]{1,0:T(8,128)S(1)} custom-call(f32[21,21]{1,0:T(8,128)S(1)} %convolution_subtract_fusion.3), custom_call_target="Cholesky" | custom-call | tf_op jit(solution)/shard_map/jit(cholesky)/cholesky | solution.py:34
  123.1 0.6 compare_reduce_fusion
  123.7 0.6 compare_reduce_fusion.1
  125.7 0.6 copy-done.5
  126.5 19.9 %custom-call.19 = f32[2,128,128]{1,2,0:T(8,128)S(1)} custom-call(f32[2,128,128]{2,1,0:T(8,128)S(1)} %pad_maximum_fusion.3), custom_call_target="InvertDiagBlocksLowerTriangular" | custom-call | tf_op jit(solution)/shard_map/jit(_cho_solve)/triangular_solve | solution.py:35
  146.4 0.8 convert_subtract_fusion.2
  147.2 0.7 fusion.7
  147.9 0.7 copy-done.2
  148.6 1.1 convolution_subtract_fusion.2
  149.7 0.3 fusion.53
  150.0 0.2 fusion.82
  150.2 0.2 copy.14
  150.4 0.1 sine_select_fusion.1
  150.5 0.8 sine_select_fusion
  151.4 0.2 broadcast_multiply_fusion
  151.6 0.1 pad.23
  151.7 2.1 %copy.19 = f32[29,8,8,256]{3,1,2,0:T(8,128)} copy(f32[29,8,8,256]{3,2,1,0:T(8,128)S(1)} %bitcast.66) | data formatting | bytes 3801088
  153.8 1.4 convolution_subtract_fusion.1
  155.2 1.1 convolution_convert_fusion
  156.3 0.9 reshape.211
  157.3 1.6 fusion.1
  158.9 1.6 fusion.83
  160.5 1.0 reshape.213
  161.5 2.6 %copy.18 = bf16[76,8,8,256]{3,1,2,0:T(8,128)(2,1)S(1)} copy(bf16[76,8,8,256]{3,2,1,0:T(8,128)(2,1)} %bitcast.14) | data formatting | bytes 4980736
  164.1 0.7 fusion.16
  164.8 1.0 multiply_reduce_fusion
  165.8 0.5 copy-done.1
  166.3 1.3 fusion
  167.6 0.1 copy.20
  167.8 0.9 slice.94
  168.7 0.6 sqrt.8
  (46 shorter events, 0.5 us)
Async XLA Ops:
  0.6 1.7 %copy-start = (bf16[19,256,256]{2,1,0:T(8,128)(2,1)S(1)}, bf16[19,256,256]{2,1,0:T(8,128)(2,1)}, u32[]{:S(2)}) copy-start(bf16[19,256,256]{2,1,0:T(8,128)(2,1)} %param.6) | copy-start | bytes 7471108
  2.3 52.1 %copy-start.10 = (s32[256]{0:T(256)}, s32[256]{0:T(256)S(1)}, u32[]{:S(2)}) copy-start(s32[256]{0:T(256)S(1)} %iota_add_fusion) | copy-start | bytes 3076
  2.3 66.0 %copy-start.9 = (s32[608,2]{0,1:T(2,128)S(1)}, s32[608,2]{0,1:T(2,128)}, u32[]{:S(2)}) copy-start(s32[608,2]{0,1:T(2,128)} %param.7) | copy-start | bytes 14596
  54.4 36.2 %all-to-all-start.1 = ((f32[32,19,225]{2,1,0:T(8,128)}), f32[32,19,225]{2,1,0:T(8,128)S(1)}, u32[]{:S(2)}, u32[]{:S(2)}) async-start(f32[32,19,225]{2,1,0:T(8,128)} %stack.2), calls=%async_computation.1 | async-start | bytes 1572864 | tf_op jit(solution)/shard_map/all_to_all | solution.py:17
  68.3 4.0 %copy-start.12 = (s32[149]{0:T(256)}, s32[149]{0:T(256)S(1)}, u32[]{:S(2)}) copy-start(s32[149]{0:T(256)S(1)} %iota_add_fusion.1) | copy-start | bytes 1792
  90.6 70.9 %all-to-all-start = ((bf16[32,19,8,256]{3,2,1,0:T(8,128)(2,1)}), bf16[32,19,8,256]{3,2,1,0:T(8,128)(2,1)}, u32[]{:S(2)}, u32[]{:S(2)}) async-start(bf16[32,19,8,256]{3,2,1,0:T(8,128)(2,1)} %copy_bitcast_fusion), calls=%async_computation | async-start | bytes 4980736 | tf_op jit(solution)/shard_map/all_to_all | solution.py:73
  96.4 0.7 copy-start.6
  125.7 0.7 copy-start.5
  146.4 3.9 %copy-start.7 = (f32[2,128,128]{1,2,0:T(8,128)}, f32[2,128,128]{1,2,0:T(8,128)S(1)}, u32[]{:S(2)}) copy-start(f32[2,128,128]{1,2,0:T(8,128)S(1)} %custom-call.19) | copy-start | bytes 393220
  147.9 0.7 copy-start.2
  151.7 2.1 %copy-start.3 = (f32[128,608]{0,1:T(8,128)S(1)}, f32[128,608]{0,1:T(8,128)}, u32[]{:S(2)}) copy-start(f32[128,608]{0,1:T(8,128)} %copy-done.2) | copy-start | bytes 933892
  151.7 3.5 %copy-start.8 = (f32[2,128,128]{1,2,0:T(8,128)S(1)}, f32[2,128,128]{1,2,0:T(8,128)}, u32[]{:S(2)}) copy-start(f32[2,128,128]{1,2,0:T(8,128)} %copy-done.7) | copy-start | bytes 393220
  151.7 5.5 %copy-start.14 = (s32[149]{0:T(256)S(1)}, s32[149]{0:T(256)}, u32[]{:S(2)}) copy-start(s32[149]{0:T(256)} %param.8) | copy-start | bytes 1792
  151.7 5.5 %copy-start.15 = (s32[225]{0:T(256)S(1)}, s32[225]{0:T(256)}, u32[]{:S(2)}) copy-start(s32[225]{0:T(256)} %constant.175.clone) | copy-start | bytes 2704
  161.5 2.6 %copy-start.4 = (bf16[128,608]{0,1:T(8,128)(2,1)S(1)}, bf16[128,608]{0,1:T(8,128)(2,1)}, u32[]{:S(2)}) copy-start(bf16[128,608]{0,1:T(8,128)(2,1)} %convolution_convert_fusion) | copy-start | bytes 466948
  164.1 0.7 copy-start.13
  164.8 1.5 copy-start.1
  164.8 1.5 copy-start.11
